TPU v7x, 8 devices: a whole 2x2x1 slice. The times are simulated.
8 devices in a mesh: replica: 1 (over z), model: 8 (over y, x, core).
Axes of the slice: x: 2, y: 2, z: 1, core: 2. Of those that a mesh axis runs over, the one named last changes fastest.
Arguments:
- x: bfloat16 [256, 4096], P('replica')
- w_query: bfloat16 [4096, 4096], P(None, 'model')
- w_key: bfloat16 [4096, 1024], replicated
- w_value: bfloat16 [4096, 1024], replicated
- w_out: bfloat16 [4096, 4096], P('model')
- k_cache: bfloat16 [256, 8, 1024, 128], P('replica')
- v_cache: bfloat16 [256, 8, 1024, 128], P('replica')
- lengths: int32 [256], P('replica')
Outputs:
- output 1: bfloat16 [256, 4096], P('replica')
- output 2: bfloat16 [256, 8, 128], P('replica')
- output 3: bfloat16 [256, 8, 128], P('replica')
All inputs are finite; a program needn't handle non-finite values.
Results may differ from a plain program's by a relative error of at most 0.00329967.
Values are sent between devices in bfloat16 or wider.
A program may use at most 4.25 GiB of HBM per device.

v0:
```python
import jax
import jax.numpy as jnp
from jax import lax
from jax.sharding import PartitionSpec as P


def attend(queries, k_rows, v_rows, k_one, v_one, seq_lens):
    inv_sqrt = queries.shape[-1] ** -0.5
    scores = jnp.einsum("bgrd,bgtd->bgrt", queries, k_rows, preferred_element_type=jnp.float32) * inv_sqrt
    score_new = jnp.einsum("bgrd,bgd->bgr", queries, k_one, preferred_element_type=jnp.float32) * inv_sqrt
    positions = jnp.arange(k_rows.shape[2])
    in_range = positions[None, None, None, :] < seq_lens[:, None, None, None]
    scores = jnp.where(in_range, scores, -jnp.inf)
    row_max = jnp.maximum(jnp.max(scores, axis=-1), score_new)
    weights = jnp.exp(scores - row_max[..., None])
    weight_new = jnp.exp(score_new - row_max)
    norm_sum = jnp.sum(weights, axis=-1) + weight_new
    out_sum = jnp.einsum("bgrt,bgtd->bgrd", weights.astype(jnp.bfloat16), v_rows, preferred_element_type=jnp.float32)
    out_sum = out_sum + weight_new.astype(jnp.bfloat16).astype(jnp.float32)[..., None] * v_one.astype(jnp.float32)[:, :, None, :]
    return (out_sum / norm_sum[..., None]).astype(jnp.bfloat16)


def solution(mesh):
    model_size = mesh.shape["model"]

    def local_step(x, w_query, w_key, w_value, w_out, k_cache, v_cache, lengths):
        batch_rows = x.shape[0]
        kv_heads = k_cache.shape[1]
        head_dim = k_cache.shape[3]
        local_rows = batch_rows // model_size
        row_start = lax.axis_index("model") * local_rows
        q_local = jnp.dot(x, w_query, preferred_element_type=jnp.float32).astype(jnp.bfloat16)
        q_rows = lax.all_to_all(q_local, "model", 0, 1, tiled=True)
        k_new = jnp.dot(x, w_key, preferred_element_type=jnp.float32).astype(jnp.bfloat16).reshape(batch_rows, kv_heads, head_dim)
        v_new = jnp.dot(x, w_value, preferred_element_type=jnp.float32).astype(jnp.bfloat16).reshape(batch_rows, kv_heads, head_dim)
        queries = q_rows.reshape(local_rows, kv_heads, -1, head_dim)
        out_rows = attend(
            queries,
            lax.dynamic_slice_in_dim(k_cache, row_start, local_rows, axis=0),
            lax.dynamic_slice_in_dim(v_cache, row_start, local_rows, axis=0),
            lax.dynamic_slice_in_dim(k_new, row_start, local_rows, axis=0),
            lax.dynamic_slice_in_dim(v_new, row_start, local_rows, axis=0),
            lax.dynamic_slice_in_dim(lengths, row_start, local_rows, axis=0),
        )
        out_heads = lax.all_to_all(out_rows.reshape(local_rows, -1), "model", 1, 0, tiled=True)
        part_sum = jnp.dot(out_heads, w_out, preferred_element_type=jnp.float32)
        full_sum = lax.psum(part_sum, "model")
        y = (x.astype(jnp.float32) + full_sum).astype(jnp.bfloat16)
        return y, k_new, v_new

    rows_spec = P("replica")
    return jax.shard_map(
        local_step,
        mesh=mesh,
        in_specs=(P("replica", None), P(None, "model"), P(), P(), P("model", None), rows_spec, rows_spec, rows_spec),
        out_specs=(rows_spec, rows_spec, rows_spec),
        check_vma=False,
    )
```

profile of v0, /device:TPU:0, one launch (start us, length us, event | category | flops | bytes accessed | tf_op | source)
XLA Modules:
  0.0 181.9 jit_solution(15746694344307922993)
XLA Ops:
  7.2 4.9 %convolution_convert_fusion.2 = bf16[256,512]{1,0:T(8,128)(2,1)} fusion(bf16[256,4096]{1,0:T(8,128)(2,1)} %param.8, bf16[4096,512]{1,0:T(8,128)(2,1)} %param.9), kind=kOutput, calls=%fused_computation.19 | convolution fusion | flops 1073872896 | bytes 6553600 | tf_op jit(solution)/shard_map/dot_general | solution.py:32
  12.1 4.3 %all-to-all-start = ((bf16[8,32,512]{2,1,0:T(8,128)(2,1)}), bf16[8,32,512]{2,1,0:T(8,128)(2,1)S(1)}, u32[]{:S(2)}, u32[]{:S(2)}) async-start(bf16[8,32,512]{2,1,0:T(8,128)(2,1)} %bitcast), calls=%async_computation | async-start | bytes 524288 | tf_op jit(solution)/shard_map/all_to_all | solution.py:33
  16.4 0.0 all-reduce.2.cloned.1.call-start
  16.5 5.8 %fusion.12 = bf16[32,8,8,128]{3,1,2,0:T(8,128)(2,1)S(1)} fusion(bf16[256,4096]{1,0:T(8,128)(2,1)S(1)} %copy-done.1, bf16[4096,1024]{1,0:T(8,128)(2,1)} %param.10), kind=kOutput, calls=%fused_computation.16 | convolution fusion | flops 2147745792 | bytes 11010048 | tf_op jit(solution)/shard_map/dot_general | solution.py:34
  22.2 0.1 copy.17
  22.3 6.0 %fusion.13 = bf16[32,8,8,128]{3,1,2,0:T(8,128)(2,1)S(1)} fusion(bf16[256,4096]{1,0:T(8,128)(2,1)S(1)} %copy-done.1, bf16[4096,1024]{1,0:T(8,128)(2,1)} %param.11), kind=kOutput, calls=%fused_computation.17 | convolution fusion | flops 2147745792 | bytes 11010048 | tf_op jit(solution)/shard_map/dot_general | solution.py:35
  28.3 0.9 copy.18
  29.2 1.5 dynamic-slice_convert_fusion
  30.7 0.1 dynamic_slice.15
  30.8 0.1 iota_compare_fusion
  30.9 0.1 reshape.54
  31.0 1.1 fusion.29
  32.0 26.1 %fusion.4 = (f32[32,8,4]{2,1,0:T(8,128)S(1)}, f32[32,8,4,1024]{3,2,1,0:T(4,128)S(1)}) fusion(pred[32,1024]{1,0:T(8,128)(4,1)S(1)} %iota_compare_fusion, bf16[256,8,1024,128]{3,2,1,0:T(8,128)(2,1)} %param.13, s32[]{:T(128)S(6)} %select_n.5, bf16[32,8,4,128]{3,2,0,1:T(4,128)(2,1)S(1)} %reshape.54), kind=kOutput, calls=%fused_computation.7 | convolution fusion | flops 271580160 | bytes 71602176 | tf_op jit(solution)/shard_map/bgrd,bgtd->bgrt/dot_general | solution.py:9
  58.2 1.1 multiply_maximum_fusion
  59.3 0.8 copy-done
  60.1 2.6 %fusion.5 = f32[32,8,4]{2,1,0:T(8,128)S(1)} fusion(f32[32,8,4,1024]{3,2,1,0:T(4,128)S(1)} %get-tuple-element.6, f32[32,8,4]{2,1,0:T(8,128)S(1)} %multiply_maximum_fusion, pred[32,1024]{1,0:T(8,128)(4,1)S(1)} %iota_compare_fusion), kind=kLoop, calls=%fused_computation.8 | loop fusion | flops 4193280 | bytes 4235264 | tf_op jit(solution)/shard_map/reduce_sum | solution.py:17
  62.8 24.4 %fusion.24 = bf16[32,8,4,128]{3,2,1,0:T(4,128)(2,1)S(1)} fusion(bf16[256,8,1024,128]{3,2,1,0:T(8,128)(2,1)} %param.14, s32[]{:T(128)S(6)} %select_n.5, f32[32,8,4,1024]{3,2,1,0:T(4,128)} %copy-done, f32[32,8,4]{2,1,0:T(8,128)S(1)} %multiply_maximum_fusion, pred[32,1024]{1,0:T(8,128)(4,1)S(1)} %iota_compare_fusion, f32[32,8,4]{2,1,0:T(8,128)S(1)} %get-tuple-element.4, ...), kind=kOutput, calls=%fused_computation.21 | convolution fusion | flops 273154048 | bytes 71741440 | tf_op jit(solution)/shard_map/bgrt,bgtd->bgrd/dot_general | solution.py:18
  87.1 0.1 all_to_all.29
  87.2 0.1 copy.13
  87.3 9.6 %all_to_all.35 = bf16[32,8,512]{2,0,1:T(8,128)(2,1)S(1)} all-to-all(bf16[32,8,512]{2,0,1:T(8,128)(2,1)S(1)} %copy.13), channel_id=1, replica_groups=mesh['replica'=1,'model'=8] {'model'}, dimensions={1} | all-to-all | bytes 524288 | tf_op jit(solution)/shard_map/all_to_all | solution.py:45
  96.9 5.4 %fusion.38 = f32[256,4096]{1,0:T(8,128)} fusion(bf16[256,512]{1,0:T(8,128)(2,1)S(1)} %bitcast.25, bf16[512,4096]{1,0:T(8,128)(2,1)} %param.12), kind=kOutput, calls=%fused_computation.37 | convolution fusion | flops 1073741824 | bytes 8650752 | tf_op jit(solution)/shard_map/dot_general | solution.py:46
  102.3 0.0 all-reduce.2.cloned.1.call-update
  102.4 68.5 %all-reduce.2.cloned.1.call-done = f32[256,4096]{1,0:T(8,128)} async-done(((f32[256,4096]{1,0:T(8,128)}), f32[256,4096]{1,0:T(8,128)}) %all-reduce.2.cloned.1.call-update) | async-done | bytes 4194320 | tf_op jit(solution)/shard_map/psum | solution.py:47
  170.9 4.1 %add_convert_fusion = bf16[256,4096]{1,0:T(8,128)(2,1)} fusion(f32[256,4096]{1,0:T(8,128)} %all-reduce.2.cloned.1.call-done, bf16[256,4096]{1,0:T(8,128)(2,1)S(1)} %copy-done.1), kind=kLoop, calls=%fused_computation.4 | loop fusion | flops 3145728 | bytes 8388608 | tf_op jit(solution)/shard_map/convert_element_type | solution.py:48
  (12 shorter events, 0.1 us)
Async XLA Ops:
  7.2 9.3 %copy-start.1 = (bf16[256,4096]{1,0:T(8,128)(2,1)S(1)}, bf16[256,4096]{1,0:T(8,128)(2,1)}, u32[]{:S(2)}) copy-start(bf16[256,4096]{1,0:T(8,128)(2,1)} %param.8) | copy-start | bytes 6291460
  12.1 18.8 %all-to-all-start = ((bf16[8,32,512]{2,1,0:T(8,128)(2,1)}), bf16[8,32,512]{2,1,0:T(8,128)(2,1)S(1)}, u32[]{:S(2)}, u32[]{:S(2)}) async-start(bf16[8,32,512]{2,1,0:T(8,128)(2,1)} %bitcast), calls=%async_computation | async-start | bytes 524288 | tf_op jit(solution)/shard_map/all_to_all | solution.py:33
  16.4 154.5 %all-reduce.2.cloned.1.call-start = ((), (), s32[]{:S(2)}) async-start(), calls=%async_computation.2 | async-start | bytes 8388608 | tf_op jit(solution)/shard_map/psum | solution.py:47
  22.3 8.4 %copy-start.2 = (bf16[32,8,8,128]{3,2,1,0:T(8,128)(2,1)}, bf16[32,8,8,128]{3,2,1,0:T(8,128)(2,1)S(1)}, u32[]{:S(2)}) copy-start(bf16[32,8,8,128]{3,2,1,0:T(8,128)(2,1)S(1)} %copy.17) | copy-start | bytes 1572868
  22.3 8.4 %copy-start.4 = (s32[256]{0:T(256)S(1)}, s32[256]{0:T(256)}, u32[]{:S(2)}) copy-start(s32[256]{0:T(256)} %param.15) | copy-start | bytes 3076
  58.2 2.0 %copy-start = (f32[32,8,4,1024]{3,2,1,0:T(4,128)}, f32[32,8,4,1024]{3,2,1,0:T(4,128)S(1)}, u32[]{:S(2)}) copy-start(f32[32,8,4,1024]{3,2,1,0:T(4,128)S(1)} %get-tuple-element.6) | copy-start | bytes 12582916
  58.2 4.6 %copy-start.3 = (f32[32,8,1,4]{3,2,1,0:T(1,128)S(1)}, f32[32,8,1,4]{3,2,1,0:T(1,128)}, u32[]{:S(2)}) copy-start(f32[32,8,1,4]{3,2,1,0:T(1,128)} %fusion.29) | copy-start | bytes 12292
Sparse Core Ops, SparseCore 0:
  102.5 68.3 all-reduce.1
where the time goes:
time: 182 us
  matrix products  73.6 us (40%)
  waiting for transfers between devices  68.6 us (38%)
  between operations  14.1 us (8%)
  blocking collectives  9.59 us (5%)
  other arithmetic  9.49 us (5%)
  starting transfers between devices  4.34 us (2%)
  local copies, waits for them, and re-layouts  2.17 us (1%)
    psum x1, waiting for transfers between devices, local_step(): full_sum = lax.psum(part_sum, 'model')  68.5 us
    dot_general x1, matrix products, attend(): jnp.einsum('bgrd,bgtd->bgrt', queries, k_rows, preferred_element_type=jnp...  26.1 us
    dot_general x1, matrix products, attend(): jnp.einsum('bgrt,bgtd->bgrd', weights.astype(jnp.bfloat16), v_rows, prefe...  24.4 us
    all_to_all x1, blocking collectives, local_step(): lax.all_to_all(out_rows.reshape(local_rows, -1), 'model', 1, 0, tiled=True)  9.59 us
    dot_general x1, matrix products, local_step(): jnp.dot(x, w_value, preferred_element_type=jnp.float32).astype(jnp.bfloat16)  5.95 us
    dot_general x1, matrix products, local_step(): jnp.dot(x, w_key, preferred_element_type=jnp.float32).astype(jnp.bfloat16)  5.76 us
    dot_general x1, matrix products, local_step(): part_sum = jnp.dot(out_heads, w_out, preferred_element_type=jnp.float32)  5.42 us
    dot_general x1, matrix products, local_step(): jnp.dot(x, w_query, preferred_element_type=jnp.float32).astype(jnp.bfloat16)  4.92 us
  transfers between devices with their start and end apart: 2, of which 1 were waited for; matrix products, arithmetic and copies ran while one was open for 8% of the time, Pallas kernels for 0%

commit v1 on v0

v1 whole, which is shorter than its diff:
```python
import functools

import jax
import jax.numpy as jnp
from jax import lax
from jax.experimental import pallas as pl
from jax.experimental.pallas import tpu as pltpu
from jax.sharding import PartitionSpec as P

BF16 = jnp.bfloat16
F32 = jnp.float32
SHORT = 32
PER_GROUP = 4
RING = 3
BLOCK = 256
K_CHUNKS = 4
CHUNK = 32
NT = (((1,), (1,)), ((), ()))


def project_and_attend_long(
    lens, x, wq, wk, wv, kc, vc,
    q_out, k1_out, v1_out, ol_out, lv_out,
    xbuf, wqbuf, wkbuf, wvbuf, kbuf, vbuf, idx, wsem, ksem, vsem,
):
    me = lax.axis_index("model")
    batch = lv_out.shape[0]
    heads, _, hd = q_out.shape
    context = kc.shape[2]
    blocks = context // BLOCK
    scale = hd ** -0.5
    depth = xbuf.shape[2]

    def loads(i):
        rows = pl.ds(i * depth, depth)
        cols = pl.ds(pl.multiple_of(me * hd, hd), hd)
        return (
            pltpu.make_async_copy(x.at[:, rows], xbuf.at[i], wsem.at[i, 0]),
            pltpu.make_async_copy(wq.at[rows, :], wqbuf.at[i], wsem.at[i, 1]),
            pltpu.make_async_copy(wk.at[rows, cols], wkbuf.at[i], wsem.at[i, 2]),
            pltpu.make_async_copy(wv.at[rows, cols], wvbuf.at[i], wsem.at[i, 3]),
        )

    for i in range(K_CHUNKS):
        for copy in loads(i):
            copy.start()

    def scan(b, n):
        length = lens[b]
        idx[n] = b
        lv_out[pl.ds(b, 1), :] = jnp.full((1, hd), length, jnp.int32)
        return n + (length > SHORT).astype(jnp.int32)

    n_long = lax.fori_loop(0, batch, scan, jnp.int32(0), unroll=8)
    n_groups = (n_long + PER_GROUP - 1) // PER_GROUP
    vbuf[...] = jnp.zeros_like(vbuf)

    def sequence(g, j):
        return idx[jnp.maximum(jnp.minimum(g * PER_GROUP + j, n_long - 1), 0)]

    def each_block(g, act):
        slot = lax.rem(g, RING)
        for j in range(PER_GROUP):
            b = sequence(g, j)
            length = lens[b]
            for t in range(blocks):
                rows = pl.ds(t * BLOCK, BLOCK)

                @pl.when(length > t * BLOCK)
                def _():
                    act(pltpu.make_async_copy(kc.at[b, me, rows, :], kbuf.at[slot, j, rows, :], ksem.at[slot, j, t]))
                    act(pltpu.make_async_copy(vc.at[b, me, rows, :], vbuf.at[slot, j, rows, :], vsem.at[slot, j, t]))

    for g in range(RING):
        @pl.when(g < n_groups)
        def _():
            each_block(jnp.int32(g), lambda copy: copy.start())

    q_acc = k_acc = v_acc = None
    for i in range(K_CHUNKS):
        for copy in loads(i):
            copy.wait()
        xs = xbuf[i]
        q_part = jnp.dot(xs, wqbuf[i], preferred_element_type=F32)
        k_part = jnp.dot(xs, wkbuf[i], preferred_element_type=F32)
        v_part = jnp.dot(xs, wvbuf[i], preferred_element_type=F32)
        for h in range(heads):
            piece = q_part[:, h * hd:(h + 1) * hd]
            q_out[h] = piece if i == 0 else q_out[h] + piece
        k1_out[...] = k_part if i == 0 else k1_out[...] + k_part
        v1_out[...] = v_part if i == 0 else v1_out[...] + v_part
    q_out[...] = q_out[...].astype(BF16).astype(F32)
    k1_out[...] = k1_out[...].astype(BF16).astype(F32)
    v1_out[...] = v1_out[...].astype(BF16).astype(F32)

    def attend(g, carry):
        slot = lax.rem(g, RING)
        each_block(g, lambda copy: copy.wait())
        results = []
        for j in range(PER_GROUP):
            b = sequence(g, j)
            length = lens[b]
            row = pl.ds(b, 1)
            q = jnp.concatenate([q_out[h, row, :] for h in range(heads)] * 2, axis=0)
            k1, v1 = k1_out[row, :], v1_out[row, :]
            s = lax.dot_general(q.astype(BF16), kbuf[slot, j], NT, preferred_element_type=F32) * scale
            s_new = jnp.sum(q * k1, axis=-1, keepdims=True) * scale
            s = jnp.where(lax.broadcasted_iota(jnp.int32, s.shape, 1) < length, s, -jnp.inf)
            m = jnp.maximum(jnp.max(s, axis=-1, keepdims=True), s_new)
            e = jnp.exp(s - m)
            e_new = jnp.exp(s_new - m)
            total = jnp.sum(e, axis=-1, keepdims=True) + e_new
            o = jnp.dot(e.astype(BF16), vbuf[slot, j], preferred_element_type=F32)
            o = (o + e_new.astype(BF16).astype(F32) * v1) / total
            results.append((row, o))
        for row, o in results:
            for h in range(heads):
                ol_out[h, row, :] = o[h:h + 1, :]

        @pl.when(g + RING < n_groups)
        def _():
            each_block(g + RING, lambda copy: copy.start())

        return carry

    lax.fori_loop(0, n_groups, attend, 0)


def attend_short_and_reduce(
    q_ref, k1_ref, v1_ref, ol_ref, lv_ref, x, wo, wk, wv, kc, vc,
    y_out, kn_out, vn_out,
    xbuf, wobuf, wkv, kbuf, vbuf, obuf, part, got_core, got_one, got_two, ybuf, kvbuf,
    load_sem, send_sem, recv_sem, store_sem,
):
    me = lax.axis_index("model")
    core = me % 2
    px = (me // 2) % 2
    py = me // 4
    flip_x = me + 2 - 4 * px
    flip_y = me + 4 - 8 * py
    other_core = 1 - core
    partner = me + 1 - 2 * core
    near_one = other_core * flip_x + core * flip_y
    near_two = other_core * flip_y + core * flip_x
    a = other_core * px + core * py
    b = other_core * py + core * px
    base = 4 * core
    mine = base + 2 * a + b
    heads, batch, hd = q_ref.shape
    width = part.shape[3]
    chunks = batch // CHUNK
    kv_width = wkv.shape[1] // 2
    kv_cols = 2 * kv_width // 8
    scale = hd ** -0.5

    loads = (
        pltpu.make_async_copy(kc.at[:, me, pl.ds(0, SHORT), :], kbuf, load_sem.at[0]),
        pltpu.make_async_copy(vc.at[:, me, pl.ds(0, SHORT), :], vbuf, load_sem.at[1]),
        pltpu.make_async_copy(wo, wobuf, load_sem.at[2]),
        pltpu.make_async_copy(x, xbuf, load_sem.at[3]),
        pltpu.make_async_copy(wk, wkv.at[:, pl.ds(0, kv_width)], load_sem.at[4]),
        pltpu.make_async_copy(wv, wkv.at[:, pl.ds(kv_width, kv_width)], load_sem.at[5]),
    )
    for copy in loads:
        copy.start()

    barrier = pltpu.get_barrier_semaphore()
    for other in (partner, near_one, near_two):
        pl.semaphore_signal(barrier, inc=1, device_id={"model": other}, device_id_type=pl.DeviceIdType.MESH)
    pl.semaphore_wait(barrier, 3)

    def send(stage, r, src, dst, other):
        return pltpu.make_async_remote_copy(
            src_ref=src, dst_ref=dst, send_sem=send_sem.at[stage, r], recv_sem=recv_sem.at[stage, r],
            device_id={"model": other}, device_id_type=pl.DeviceIdType.MESH,
        )

    def rows_of(r):
        return pl.ds(pl.multiple_of(r * CHUNK, CHUNK), CHUNK)

    def cols_of(f, count):
        return pl.ds(pl.multiple_of(f * width, width), count * width)

    def to_core(r):
        return send(0, r, part.at[r, pl.ds(4 * other_core, 4)], got_core.at[r], partner)

    def to_one(r):
        return send(1, r, part.at[r, pl.ds(base + 2 * (1 - a), 2)], got_one.at[r], near_one)

    def to_two(r):
        return send(2, r, part.at[r, base + 2 * a + 1 - b], got_two.at[r], near_two)

    def y_to_two(r):
        view = ybuf.at[rows_of(r), cols_of(mine, 1)]
        return send(3, r, view, view, near_two)

    def y_to_one(r):
        view = ybuf.at[rows_of(r), cols_of(base + 2 * a, 2)]
        return send(4, r, view, view, near_one)

    def y_to_core(r):
        view = ybuf.at[rows_of(r), cols_of(base, 4)]
        return send(5, r, view, view, partner)

    def y_store(r):
        return pltpu.make_async_copy(ybuf.at[rows_of(r), :], y_out.at[rows_of(r), :], store_sem.at[r])

    def attend(r):
        for g in range(CHUNK // 8):
            rows = pl.ds(pl.multiple_of(r * CHUNK + g * 8, 8), 8)
            q = jnp.concatenate([q_ref[h, rows, :] for h in range(heads)], axis=0)
            k1 = jnp.concatenate([k1_ref[rows, :]] * heads, axis=0)
            v1 = jnp.concatenate([v1_ref[rows, :]] * heads, axis=0)
            lens = jnp.concatenate([lv_ref[rows, :]] * heads, axis=0)
            k = kbuf[rows].reshape(8 * SHORT, hd)
            v = vbuf[rows].reshape(8 * SHORT, hd)
            s = lax.dot_general(q.astype(BF16), k, NT, preferred_element_type=F32) * scale
            s_new = jnp.sum(q * k1, axis=-1, keepdims=True) * scale
            lane = lax.broadcasted_iota(jnp.int32, s.shape, 1)
            line = lax.broadcasted_iota(jnp.int32, s.shape, 0)
            slot = lane - (line % 8) * SHORT
            wide = jnp.concatenate([lens] * (s.shape[1] // hd), axis=1)
            s = jnp.where((slot >= 0) & (slot < jnp.minimum(wide, SHORT)), s, -jnp.inf)
            m = jnp.maximum(jnp.max(s, axis=-1, keepdims=True), s_new)
            e = jnp.exp(s - m)
            e_new = jnp.exp(s_new - m)
            total = jnp.sum(e, axis=-1, keepdims=True) + e_new
            o = jnp.dot(e.astype(BF16), v, preferred_element_type=F32)
            o = (o + e_new.astype(BF16).astype(F32) * v1) / total
            for h in range(heads):
                picked = jnp.where(lens[:8] > SHORT, ol_ref[h, rows, :], o[h * 8:(h + 1) * 8])
                obuf[pl.ds(g * 8, 8), pl.ds(h * hd, hd)] = picked

        o_rows = obuf[...].astype(BF16)

        def piece(f, carry):
            part[r, f] = jnp.dot(o_rows, wobuf[:, cols_of(f, 1)], preferred_element_type=F32)
            return carry

        lax.fori_loop(0, 8, piece, 0)

    def new_rows(t):
        cols = pl.ds(pl.multiple_of(t * kv_cols, kv_cols), kv_cols)
        kvbuf[:, cols] = jnp.dot(xbuf[...], wkv[:, cols], preferred_element_type=F32).astype(BF16)

    for copy in loads[:4]:
        copy.wait()

    def step(t, carry):
        @pl.when((t >= 6) & (t < chunks + 6))
        def _():
            y_to_core(t - 6).wait()
            y_store(t - 6).start()

        @pl.when((t >= 5) & (t < chunks + 5))
        def _():
            y_to_one(t - 5).wait()
            y_to_core(t - 5).start()

        @pl.when((t >= 4) & (t < chunks + 4))
        def _():
            y_to_two(t - 4).wait()
            y_to_one(t - 4).start()

        @pl.when((t >= 3) & (t < chunks + 3))
        def _():
            r = t - 3
            to_two(r).wait()
            total = part[r, mine] + got_two[r]
            total = total + xbuf[rows_of(r), cols_of(mine, 1)].astype(F32)
            ybuf[rows_of(r), cols_of(mine, 1)] = total.astype(BF16)
            y_to_two(r).start()

        @pl.when((t >= 2) & (t < chunks + 2))
        def _():
            r = t - 2
            to_one(r).wait()
            part[r, pl.ds(base + 2 * a, 2)] += got_one[r]
            to_two(r).start()

        @pl.when((t >= 1) & (t < chunks + 1))
        def _():
            r = t - 1
            to_core(r).wait()
            part[r, pl.ds(base, 4)] += got_core[r]
            to_one(r).start()

        @pl.when(t < chunks)
        def _():
            attend(t)
            to_core(t).start()

        @pl.when(t == 3)
        def _():
            loads[4].wait()
            loads[5].wait()

        @pl.when((t >= 3) & (t < 11))
        def _():
            new_rows(t - 3)

        return carry

    lax.fori_loop(0, chunks + 6, step, 0)
    k_store = pltpu.make_async_copy(kvbuf.at[:, pl.ds(0, kv_width)], kn_out, load_sem.at[0])
    v_store = pltpu.make_async_copy(kvbuf.at[:, pl.ds(kv_width, kv_width)], vn_out, load_sem.at[1])
    k_store.start()
    v_store.start()
    for r in range(chunks):
        y_store(r).wait()
    k_store.wait()
    v_store.wait()


def solution(mesh):
    def local_step(x, w_query, w_key, w_value, w_out, k_cache, v_cache, lengths):
        batch, width = x.shape
        kv_heads, context, hd = k_cache.shape[1:]
        heads = w_query.shape[1] // hd
        kv_width = kv_heads * hd
        depth = width // K_CHUNKS
        piece = width // 8
        chunks = batch // CHUNK
        vmem = pl.BlockSpec(memory_space=pltpu.VMEM)
        hbm = pl.BlockSpec(memory_space=pl.ANY)
        sds = jax.ShapeDtypeStruct

        q, k1, v1, ol, lv = pl.pallas_call(
            project_and_attend_long,
            out_shape=(
                sds((heads, batch, hd), F32), sds((batch, hd), F32), sds((batch, hd), F32),
                sds((heads, batch, hd), F32), sds((batch, hd), jnp.int32),
            ),
            in_specs=[pl.BlockSpec(memory_space=pltpu.SMEM)] + [hbm] * 6,
            out_specs=[vmem] * 5,
            scratch_shapes=[
                pltpu.VMEM((K_CHUNKS, batch, depth), BF16),
                pltpu.VMEM((K_CHUNKS, depth, heads * hd), BF16),
                pltpu.VMEM((K_CHUNKS, depth, hd), BF16),
                pltpu.VMEM((K_CHUNKS, depth, hd), BF16),
                pltpu.VMEM((RING, PER_GROUP, context, hd), BF16),
                pltpu.VMEM((RING, PER_GROUP, context, hd), BF16),
                pltpu.SMEM((batch,), jnp.int32),
                pltpu.SemaphoreType.DMA((K_CHUNKS, 4)),
                pltpu.SemaphoreType.DMA((RING, PER_GROUP, context // BLOCK)),
                pltpu.SemaphoreType.DMA((RING, PER_GROUP, context // BLOCK)),
            ],
            compiler_params=pltpu.CompilerParams(vmem_limit_bytes=48 * 2**20),
            name="project_and_attend_long",
        )(lengths, x, w_query, w_key, w_value, k_cache, v_cache)

        y, kn, vn = pl.pallas_call(
            attend_short_and_reduce,
            out_shape=(sds((batch, width), BF16), sds((batch, kv_width), BF16), sds((batch, kv_width), BF16)),
            in_specs=[vmem] * 5 + [hbm] * 6,
            out_specs=[hbm] * 3,
            scratch_shapes=[
                pltpu.VMEM((batch, width), BF16),
                pltpu.VMEM((heads * hd, width), BF16),
                pltpu.VMEM((width, 2 * kv_width), BF16),
                pltpu.VMEM((batch, SHORT, hd), BF16),
                pltpu.VMEM((batch, SHORT, hd), BF16),
                pltpu.VMEM((CHUNK, heads * hd), F32),
                pltpu.VMEM((chunks, 8, CHUNK, piece), F32),
                pltpu.VMEM((chunks, 4, CHUNK, piece), F32),
                pltpu.VMEM((chunks, 2, CHUNK, piece), F32),
                pltpu.VMEM((chunks, CHUNK, piece), F32),
                pltpu.VMEM((batch, width), BF16),
                pltpu.VMEM((batch, 2 * kv_width), BF16),
                pltpu.SemaphoreType.DMA((6,)),
                pltpu.SemaphoreType.DMA((6, chunks)),
                pltpu.SemaphoreType.DMA((6, chunks)),
                pltpu.SemaphoreType.DMA((chunks,)),
            ],
            compiler_params=pltpu.CompilerParams(
                vmem_limit_bytes=60 * 2**20, collective_id=0, has_side_effects=True
            ),
            name="attend_short_and_reduce",
        )(q, k1, v1, ol, lv, x, w_out, w_key, w_value, k_cache, v_cache)
        return y, kn.reshape(batch, kv_heads, hd), vn.reshape(batch, kv_heads, hd)

    rows_spec = P("replica")
    return jax.shard_map(
        local_step,
        mesh=mesh,
        in_specs=(P("replica", None), P(None, "model"), P(), P(), P("model", None), rows_spec, rows_spec, rows_spec),
        out_specs=(rows_spec, rows_spec, rows_spec),
        check_vma=False,
    )
```

time: 182 us -> 86.8 us (0.48)
  matrix products: 73.6 us -> 0 us
  Pallas kernels: 0 us -> 73 us
  waiting for transfers between devices: 68.6 us -> 0 us
  between operations: 14.1 us -> 0.67 us
  local copies, waits for them, and re-layouts: 2.17 us -> 12.8 us
  blocking collectives: 9.59 us -> 0 us
  other arithmetic: 9.49 us -> 0 us
  starting transfers between devices: 4.34 us -> 0 us
    dot_general x7 -> x0, matrix products: 73.6 us -> none  [the longest x1 26.1 us: attend(): jnp.einsum('bgrd,bgtd->bgrt', queries, k_rows, preferred_element_type=jnp...]
    pallas_call x0 -> x2, Pallas kernels: none -> 73 us  [the longest x1 60.3 us: local_step(): pl.pallas_call(attend_short_and_reduce, out_shape=(sds((batch, width), BF...]
    psum x1 -> x0, waiting for transfers between devices: 68.5 us -> none  [local_step(): full_sum = lax.psum(part_sum, 'model')]
    unnamed x12 -> x17, local copies, waits for them, and re-layouts: 1.84 us -> 12.8 us
    all_to_all x1 -> x0, blocking collectives: 9.59 us -> none  [local_step(): lax.all_to_all(out_rows.reshape(local_rows, -1), 'model', 1, 0, tiled=True)]
    convert_element_type x3 -> x0, other arithmetic: 5.68 us -> none  [the longest x1 4.14 us: local_step(): y = (x.astype(jnp.float32) + full_sum).astype(jnp.bfloat16)]
    all_to_all x1 -> x0, starting transfers between devices: 4.3 us -> none  [local_step(): q_rows = lax.all_to_all(q_local, 'model', 0, 1, tiled=True)]
    reduce_sum x1 -> x0, other arithmetic: 2.61 us -> none  [attend(): norm_sum = jnp.sum(weights, axis=-1) + weight_new]
  transfers between devices with their start and end apart: 2 -> 0, of which waited for: 1 -> 0; matrix products, arithmetic and copies ran while one was open for 8% -> 0% of each run, Pallas kernels for 0% -> 0%
where the time goes in v1:
time: 86.8 us; the launch traced here: 86.5 us
  Pallas kernels  73 us (84%)
  local copies, waits for them, and re-layouts  12.8 us (15%)
    pallas_call x1, Pallas kernels, local_step(): pl.pallas_call(attend_short_and_reduce, out_shape=(sds((batch, width), BF...  60.3 us
    unnamed x17, local copies, waits for them, and re-layouts  12.8 us
    pallas_call x1, Pallas kernels, local_step(): pl.pallas_call(project_and_attend_long, out_shape=(sds((heads, batch, hd)...  12.7 us

profile of v1, /device:TPU:0, one launch (start us, length us, event | category | flops | bytes accessed | tf_op | source)
XLA Modules:
  0.0 86.5 jit_solution(4105089870424456565)
XLA Ops:
  0.6 0.0 copy-start
  0.6 1.6 %copy-done = bf16[256,4096]{1,0:T(8,128)(2,1)S(1)} copy-done((bf16[256,4096]{1,0:T(8,128)(2,1)S(1)}, bf16[256,4096]{1,0:T(8,128)(2,1)}, u32[]{:S(2)}) %copy-start) | copy-done | bytes 2097176
  2.2 0.0 copy-start.6
  2.2 0.7 copy-done.6
  2.9 12.7 %project_and_attend_long.1 = (f32[4,256,128]{2,1,0:T(8,128)S(1)}, f32[256,128]{1,0:T(8,128)S(1)}, f32[256,128]{1,0:T(8,128)S(1)}, f32[4,256,128]{2,1,0:T(8,128)S(1)}, s32[256,128]{1,0:T(8,128)S(1)}) custom-call(s32[256]{0:T(256)S(1)} %copy-done.6, bf16[256,4096]{1,0:T(8,128)(2,1)S(1)} %copy-done, bf16[4096,512]{1,0:T(8,128)(2,1)} %wq.1, ...), custom_call_target="tpu_custom_call" | custom-call | tf_op jit(solution)/shard_map/project_and_attend_long/pallas_call | solution.py:328
  15.7 0.0 copy-start.1
  15.7 0.8 copy-done.1
  16.5 0.0 copy-start.2
  16.5 0.8 copy-done.2
  17.2 0.0 copy-start.3
  17.3 0.7 copy-done.3
  17.9 0.0 copy-start.4
  17.9 0.6 copy-done.4
  18.6 0.0 copy-start.5
  18.6 0.7 copy-done.5
  19.2 60.3 %attend_short_and_reduce.1 = (bf16[256,4096]{1,0:T(8,128)(2,1)}, bf16[256,1024]{1,0:T(8,128)(2,1)}, bf16[256,1024]{1,0:T(8,128)(2,1)}) custom-call(f32[4,256,128]{2,1,0:T(8,128)} %copy-done.1, f32[256,128]{1,0:T(8,128)} %copy-done.3, f32[256,128]{1,0:T(8,128)} %copy-done.4, f32[4,256,128]{2,1,0:T(8,128)} %copy-done.2, s32[256,128]{1,0:T(8,128)} %copy-done.5, ...), custom_call_target="tpu_custom_call" | custom-call | tf_op jit(solution)/shard_map/attend_short_and_reduce/pallas_call | solution.py:352
  79.5 1.9 %copy.11 = bf16[32,8,8,128]{3,2,1,0:T(8,128)(2,1)} copy(bf16[32,8,8,128]{3,1,2,0:T(8,128)(2,1)} %bitcast.7) | data formatting | bytes 1048576
  81.4 1.9 %copy.12 = bf16[32,8,8,128]{3,2,1,0:T(8,128)(2,1)} copy(bf16[32,8,8,128]{3,1,2,0:T(8,128)(2,1)} %bitcast.6) | data formatting | bytes 1048576
  83.4 3.1 %copy.14 = bf16[256,4096]{1,0:T(8,128)(2,1)} copy(bf16[256,4096]{1,0:T(8,128)(2,1)} %get-tuple-element.22) | data formatting | bytes 4194304
Async XLA Ops:
  0.6 1.6 %copy-start = (bf16[256,4096]{1,0:T(8,128)(2,1)S(1)}, bf16[256,4096]{1,0:T(8,128)(2,1)}, u32[]{:S(2)}) copy-start(bf16[256,4096]{1,0:T(8,128)(2,1)} %x.3) | copy-start | bytes 6291460
  2.2 0.7 copy-start.6
  15.7 0.8 copy-start.1
  16.5 0.8 copy-start.2
  17.2 0.7 copy-start.3
  17.9 0.6 copy-start.4
  18.6 0.7 copy-start.5

commit v2 on v1

v2 whole, which is shorter than its diff:
```python
import functools

import jax
import jax.numpy as jnp
from jax import lax
from jax.experimental import pallas as pl
from jax.experimental.pallas import tpu as pltpu
from jax.sharding import PartitionSpec as P

BF16 = jnp.bfloat16
F32 = jnp.float32
SHORT = 32
PER_GROUP = 4
RING = 3
BLOCK = 256
K_CHUNKS = 4
BLOCK_ROWS = 64
KV_STEPS = 8
PARTS = ((0, 64), (64, 192))
CHUNKS = tuple((32 * i, 32) for i in range(8))
ATTEND, PROJECT, NEW = 6, 7, 8
ORDER = (
    (ATTEND, 0), (PROJECT, 0), (ATTEND, 1), (0, 0), (0, 1), (PROJECT, 1),
    (0, 2), (1, 0), (0, 3), (0, 4), (NEW, 0), (0, 5), (1, 1), (0, 6), (0, 7), (NEW, 1), (2, 0), (NEW, 2),
    (1, 2), (2, 1), (NEW, 3), (1, 3), (3, 0), (NEW, 4), (1, 4), (2, 2), (3, 1), (2, 3), (NEW, 5), (1, 5), (2, 4),
    (3, 2), (3, 3), (NEW, 6), (1, 6), (2, 5), (3, 4), (NEW, 7), (1, 7), (2, 6), (4, 0), (3, 5), (4, 1), (5, 0),
    (2, 7), (5, 1), (4, 2), (3, 6), (4, 3), (5, 2), (4, 4), (5, 3), (3, 7), (4, 5), (5, 4), (4, 6), (5, 5),
    (5, 6), (4, 7), (5, 7),
)
NT = (((1,), (1,)), ((), ()))


def project_and_attend_long(
    lens_hbm, x, wq, wk, wv, wo, kc, vc,
    q_out, k1_out, v1_out, ol_out, lv_out, ks_out, vs_out, wo_out,
    xbuf, wqbuf, wkbuf, wvbuf, kbuf, vbuf, lens, idx, wsem, ksem, vsem, next_sem,
):
    me = lax.axis_index("model")
    batch = lv_out.shape[0]
    heads, _, hd = q_out.shape
    context = kc.shape[2]
    blocks = context // BLOCK
    scale = hd ** -0.5
    depth = xbuf.shape[2]

    def loads(i):
        rows = pl.ds(i * depth, depth)
        cols = pl.ds(pl.multiple_of(me * hd, hd), hd)
        return (
            pltpu.make_async_copy(x.at[:, rows], xbuf.at[i], wsem.at[i, 0]),
            pltpu.make_async_copy(wq.at[rows, :], wqbuf.at[i], wsem.at[i, 1]),
            pltpu.make_async_copy(wk.at[rows, cols], wkbuf.at[i], wsem.at[i, 2]),
            pltpu.make_async_copy(wv.at[rows, cols], wvbuf.at[i], wsem.at[i, 3]),
        )

    lens_load = pltpu.make_async_copy(lens_hbm, lens, wsem.at[0, 4])
    lens_load.start()
    for i in range(K_CHUNKS):
        for copy in loads(i):
            copy.start()
    lens_load.wait()

    def scan(b, n):
        length = lens[b]
        idx[n] = b
        lv_out[pl.ds(b, 1), :] = jnp.full((1, hd), length, jnp.int32)
        return n + (length > SHORT).astype(jnp.int32)

    n_long = lax.fori_loop(0, batch, scan, jnp.int32(0), unroll=8)
    n_groups = (n_long + PER_GROUP - 1) // PER_GROUP
    vbuf[...] = jnp.zeros_like(vbuf)

    def sequence(g, j):
        return idx[jnp.maximum(jnp.minimum(g * PER_GROUP + j, n_long - 1), 0)]

    def each_block(g, act):
        slot = lax.rem(g, RING)
        for j in range(PER_GROUP):
            b = sequence(g, j)
            length = lens[b]
            for t in range(blocks):
                rows = pl.ds(t * BLOCK, BLOCK)

                @pl.when(length > t * BLOCK)
                def _():
                    act(pltpu.make_async_copy(kc.at[b, me, rows, :], kbuf.at[slot, j, rows, :], ksem.at[slot, j, t]))
                    act(pltpu.make_async_copy(vc.at[b, me, rows, :], vbuf.at[slot, j, rows, :], vsem.at[slot, j, t]))

    for g in range(RING):
        @pl.when(g < n_groups)
        def _():
            each_block(jnp.int32(g), lambda copy: copy.start())

    ahead = (
        pltpu.make_async_copy(kc.at[:, me, pl.ds(0, SHORT), :], ks_out, next_sem.at[0]),
        pltpu.make_async_copy(vc.at[:, me, pl.ds(0, SHORT), :], vs_out, next_sem.at[1]),
        pltpu.make_async_copy(wo, wo_out, next_sem.at[2]),
    )
    for copy in ahead:
        copy.start()

    for i in range(K_CHUNKS):
        for copy in loads(i):
            copy.wait()
        xs = xbuf[i]
        q_part = jnp.dot(xs, wqbuf[i], preferred_element_type=F32)
        k_part = jnp.dot(xs, wkbuf[i], preferred_element_type=F32)
        v_part = jnp.dot(xs, wvbuf[i], preferred_element_type=F32)
        for h in range(heads):
            piece = q_part[:, h * hd:(h + 1) * hd]
            q_out[h] = piece if i == 0 else q_out[h] + piece
        k1_out[...] = k_part if i == 0 else k1_out[...] + k_part
        v1_out[...] = v_part if i == 0 else v1_out[...] + v_part
    q_out[...] = q_out[...].astype(BF16).astype(F32)
    k1_out[...] = k1_out[...].astype(BF16).astype(F32)
    v1_out[...] = v1_out[...].astype(BF16).astype(F32)

    def attend(g, carry):
        slot = lax.rem(g, RING)
        each_block(g, lambda copy: copy.wait())
        results = []
        for j in range(PER_GROUP):
            b = sequence(g, j)
            length = lens[b]
            row = pl.ds(b, 1)
            q = jnp.concatenate([q_out[h, row, :] for h in range(heads)] * 2, axis=0)
            k1, v1 = k1_out[row, :], v1_out[row, :]
            s = lax.dot_general(q.astype(BF16), kbuf[slot, j], NT, preferred_element_type=F32) * scale
            s_new = jnp.sum(q * k1, axis=-1, keepdims=True) * scale
            s = jnp.where(lax.broadcasted_iota(jnp.int32, s.shape, 1) < length, s, -jnp.inf)
            m = jnp.maximum(jnp.max(s, axis=-1, keepdims=True), s_new)
            e = jnp.exp(s - m)
            e_new = jnp.exp(s_new - m)
            total = jnp.sum(e, axis=-1, keepdims=True) + e_new
            o = jnp.dot(e.astype(BF16), vbuf[slot, j], preferred_element_type=F32)
            o = (o + e_new.astype(BF16).astype(F32) * v1) / total
            results.append((row, o))
        for row, o in results:
            for h in range(heads):
                ol_out[h, row, :] = o[h:h + 1, :]

        @pl.when(g + RING < n_groups)
        def _():
            each_block(g + RING, lambda copy: copy.start())

        return carry

    lax.fori_loop(0, n_groups, attend, 0)
    for copy in ahead:
        copy.wait()


def attend_short_and_reduce(
    q_ref, k1_ref, v1_ref, ol_ref, lv_ref, kbuf, vbuf, wobuf, x, wk, wv,
    y_out, kn_out, vn_out,
    xbuf, wkv, obuf, part, got_core, got_one, got_two, kvbuf,
    load_sem, send_sem, recv_sem,
):
    me = lax.axis_index("model")
    core = me % 2
    px = (me // 2) % 2
    py = me // 4
    flip_x = me + 2 - 4 * px
    flip_y = me + 4 - 8 * py
    other_core = 1 - core
    partner = me + 1 - 2 * core
    near_one = other_core * flip_x + core * flip_y
    near_two = other_core * flip_y + core * flip_x
    a = other_core * px + core * py
    b = other_core * py + core * px
    base = 4 * core
    mine = base + 2 * a + b
    heads, batch, hd = q_ref.shape
    width = part.shape[2]
    kv_width = wkv.shape[1] // 2
    kv_heads = kv_width // hd
    slice_heads = 2 * kv_heads // KV_STEPS
    scale = hd ** -0.5

    loads = (
        pltpu.make_async_copy(x, xbuf, load_sem.at[0]),
        pltpu.make_async_copy(wk, wkv.at[:, pl.ds(0, kv_width)], load_sem.at[1]),
        pltpu.make_async_copy(wv, wkv.at[:, pl.ds(kv_width, kv_width)], load_sem.at[2]),
    )
    for copy in loads:
        copy.start()

    barrier = pltpu.get_barrier_semaphore()
    for other in (partner, near_one, near_two):
        pl.semaphore_signal(barrier, inc=1, device_id={"model": other}, device_id_type=pl.DeviceIdType.MESH)

    def rows_of(r):
        first, count = CHUNKS[r]
        return pl.ds(first, count)

    def cols_of(f, count):
        return pl.ds(pl.multiple_of(f * width, width), count * width)

    def send(stage, r):
        rows = rows_of(r)
        if stage == 0:
            src, dst, other = part.at[pl.ds(4 * other_core, 4), rows], got_core.at[:, rows], partner
        elif stage == 1:
            src, dst, other = part.at[pl.ds(base + 2 * (1 - a), 2), rows], got_one.at[:, rows], near_one
        elif stage == 2:
            src, dst, other = part.at[base + 2 * a + 1 - b, rows], got_two.at[rows], near_two
        elif stage == 3:
            src = dst = y_out.at[rows, cols_of(mine, 1)]
            other = near_two
        elif stage == 4:
            src = dst = y_out.at[rows, cols_of(base + 2 * a, 2)]
            other = near_one
        else:
            src = dst = y_out.at[rows, cols_of(base, 4)]
            other = partner
        return pltpu.make_async_remote_copy(
            src_ref=src, dst_ref=dst, send_sem=send_sem.at[stage, r], recv_sem=recv_sem.at[stage, r],
            device_id={"model": other}, device_id_type=pl.DeviceIdType.MESH,
        )

    def advance(stage, r):
        rows = rows_of(r)
        send(stage, r).wait()
        if stage == 0:
            part[pl.ds(base, 4), rows] += got_core[:, rows]
        elif stage == 1:
            part[pl.ds(base + 2 * a, 2), rows] += got_one[:, rows]
        elif stage == 2:
            total = part[mine, rows] + got_two[rows]
            total = total + xbuf[rows, cols_of(mine, 1)].astype(F32)
            y_out[rows, cols_of(mine, 1)] = total.astype(BF16)
        if stage < 5:
            send(stage + 1, r).start()

    def attend_block(first):
        for g in range(BLOCK_ROWS // 8):
            rows = pl.ds(pl.multiple_of(first + g * 8, 8), 8)
            q = jnp.concatenate([q_ref[h, rows, :] for h in range(heads)], axis=0)
            k1 = jnp.concatenate([k1_ref[rows, :]] * heads, axis=0)
            v1 = jnp.concatenate([v1_ref[rows, :]] * heads, axis=0)
            lens = jnp.concatenate([lv_ref[rows, :]] * heads, axis=0)
            k = kbuf[rows].reshape(8 * SHORT, hd)
            v = vbuf[rows].reshape(8 * SHORT, hd)
            s = lax.dot_general(q.astype(BF16), k, NT, preferred_element_type=F32) * scale
            s_new = jnp.sum(q * k1, axis=-1, keepdims=True) * scale
            lane = lax.broadcasted_iota(jnp.int32, s.shape, 1)
            line = lax.broadcasted_iota(jnp.int32, s.shape, 0)
            slot = lane - (line % 8) * SHORT
            wide = jnp.concatenate([lens] * (s.shape[1] // hd), axis=1)
            s = jnp.where((slot >= 0) & (slot < jnp.minimum(wide, SHORT)), s, -jnp.inf)
            m = jnp.maximum(jnp.max(s, axis=-1, keepdims=True), s_new)
            e = jnp.exp(s - m)
            e_new = jnp.exp(s_new - m)
            total = jnp.sum(e, axis=-1, keepdims=True) + e_new
            o = jnp.dot(e.astype(BF16), v, preferred_element_type=F32)
            o = (o + e_new.astype(BF16).astype(F32) * v1) / total
            for h in range(heads):
                picked = jnp.where(lens[:8] > SHORT, ol_ref[h, rows, :], o[h * 8:(h + 1) * 8])
                obuf[rows, pl.ds(h * hd, hd)] = picked

    def attend(first, count):
        if count == BLOCK_ROWS:
            attend_block(first)
        else:
            def body(i, carry):
                attend_block(first + i * BLOCK_ROWS)
                return carry

            lax.fori_loop(0, count // BLOCK_ROWS, body, 0)

    def project_out(first, count):
        rows = pl.ds(first, count)
        o_rows = obuf[rows, :].astype(BF16)
        for f in range(8):
            part[f, rows] = jnp.dot(o_rows, wobuf[:, f * width:(f + 1) * width], preferred_element_type=F32)

    def new_rows(t):
        if t == 0:
            loads[0].wait()
            loads[1].wait()
            loads[2].wait()
        cols = pl.ds(t * slice_heads * hd, slice_heads * hd)
        fresh = jnp.dot(xbuf[...], wkv[:, cols], preferred_element_type=F32)
        for h in range(slice_heads):
            kvbuf[:, (t * slice_heads + h) % kv_heads, :] = fresh[:, h * hd:(h + 1) * hd]
        if t == KV_STEPS // 2 - 1:
            kn_out[...] = kvbuf[...].astype(BF16)
        if t == KV_STEPS - 1:
            vn_out[...] = kvbuf[...].astype(BF16)

    for op, i in ORDER:
        if op == ATTEND:
            attend(*PARTS[i])
        elif op == PROJECT:
            project_out(*PARTS[i])
            if i == 0:
                pl.semaphore_wait(barrier, 3)
            for r, (first, _) in enumerate(CHUNKS):
                if PARTS[i][0] <= first < PARTS[i][0] + PARTS[i][1]:
                    send(0, r).start()
        elif op == NEW:
            new_rows(i)
        else:
            advance(op, i)


def copy_out(y, kn, vn, y_out, kn_out, vn_out, sem):
    copies = [
        pltpu.make_async_copy(src, dst, sem.at[i])
        for i, (src, dst) in enumerate(((y, y_out), (kn, kn_out), (vn, vn_out)))
    ]
    for copy in copies:
        copy.start()
    for copy in copies:
        copy.wait()


def solution(mesh):
    def local_step(x, w_query, w_key, w_value, w_out, k_cache, v_cache, lengths):
        batch, width = x.shape
        kv_heads, context, hd = k_cache.shape[1:]
        heads = w_query.shape[1] // hd
        kv_width = kv_heads * hd
        depth = width // K_CHUNKS
        piece = width // 8
        vmem = pl.BlockSpec(memory_space=pltpu.VMEM)
        hbm = pl.BlockSpec(memory_space=pltpu.HBM)
        sds = jax.ShapeDtypeStruct
        x, w_query, w_key, w_value, w_out, k_cache, v_cache, lengths = (
            pltpu.with_memory_space_constraint(array, pltpu.HBM)
            for array in (x, w_query, w_key, w_value, w_out, k_cache, v_cache, lengths)
        )

        ahead = pl.pallas_call(
            project_and_attend_long,
            out_shape=(
                sds((heads, batch, hd), F32), sds((batch, hd), F32), sds((batch, hd), F32),
                sds((heads, batch, hd), F32), sds((batch, hd), jnp.int32),
                sds((batch, SHORT, hd), BF16), sds((batch, SHORT, hd), BF16), sds((heads * hd, width), BF16),
            ),
            in_specs=[hbm] * 8,
            out_specs=[vmem] * 8,
            scratch_shapes=[
                pltpu.VMEM((K_CHUNKS, batch, depth), BF16),
                pltpu.VMEM((K_CHUNKS, depth, heads * hd), BF16),
                pltpu.VMEM((K_CHUNKS, depth, hd), BF16),
                pltpu.VMEM((K_CHUNKS, depth, hd), BF16),
                pltpu.VMEM((RING, PER_GROUP, context, hd), BF16),
                pltpu.VMEM((RING, PER_GROUP, context, hd), BF16),
                pltpu.SMEM((batch,), jnp.int32),
                pltpu.SMEM((batch,), jnp.int32),
                pltpu.SemaphoreType.DMA((K_CHUNKS, 5)),
                pltpu.SemaphoreType.DMA((RING, PER_GROUP, context // BLOCK)),
                pltpu.SemaphoreType.DMA((RING, PER_GROUP, context // BLOCK)),
                pltpu.SemaphoreType.DMA((3,)),
            ],
            compiler_params=pltpu.CompilerParams(vmem_limit_bytes=32 * 2**20),
            name="project_and_attend_long",
        )(lengths, x, w_query, w_key, w_value, w_out, k_cache, v_cache)

        new_shape = (batch, kv_heads, hd)
        result = (sds((batch, width), BF16), sds(new_shape, BF16), sds(new_shape, BF16))
        held = pl.pallas_call(
            attend_short_and_reduce,
            out_shape=result,
            in_specs=[vmem] * 8 + [hbm] * 3,
            out_specs=[vmem] * 3,
            scratch_shapes=[
                pltpu.VMEM((batch, width), BF16),
                pltpu.VMEM((width, 2 * kv_width), BF16),
                pltpu.VMEM((batch, heads * hd), F32),
                pltpu.VMEM((8, batch, piece), F32),
                pltpu.VMEM((4, batch, piece), F32),
                pltpu.VMEM((2, batch, piece), F32),
                pltpu.VMEM((batch, piece), F32),
                pltpu.VMEM(new_shape, F32),
                pltpu.SemaphoreType.DMA((3,)),
                pltpu.SemaphoreType.DMA((6, len(CHUNKS))),
                pltpu.SemaphoreType.DMA((6, len(CHUNKS))),
            ],
            compiler_params=pltpu.CompilerParams(
                vmem_limit_bytes=40 * 2**20, collective_id=0, has_side_effects=True
            ),
            name="attend_short_and_reduce",
        )(*ahead, x, w_key, w_value)
        return pl.pallas_call(
            copy_out,
            out_shape=result,
            in_specs=[vmem] * 3,
            out_specs=[pl.BlockSpec(memory_space=pltpu.HBM)] * 3,
            scratch_shapes=[pltpu.SemaphoreType.DMA((3,))],
            compiler_params=pltpu.CompilerParams(vmem_limit_bytes=2**20),
            name="copy_out",
        )(*held)

    rows_spec = P("replica")
    return jax.shard_map(
        local_step,
        mesh=mesh,
        in_specs=(P("replica", None), P(None, "model"), P(), P(), P("model", None), rows_spec, rows_spec, rows_spec),
        out_specs=(rows_spec, rows_spec, rows_spec),
        check_vma=False,
    )
```

time: 86.8 us -> 60.9 us (0.70)
  Pallas kernels: 73 us -> 60 us
  local copies, waits for them, and re-layouts: 12.8 us -> 0 us
    pallas_call x1 -> x2, Pallas kernels: 60.3 us -> 47.1 us  [the longest x1 45.4 us: local_step(): pl.pallas_call(attend_short_and_reduce, out_shape=result, in_specs=[vmem]...]
    unnamed x17 -> x0, local copies, waits for them, and re-layouts: 12.8 us -> none
where the time goes in v2:
time: 60.9 us; the launch traced here: 60.8 us
  Pallas kernels  60 us (99%)
  between operations  0.81 us (1%)
    pallas_call x1, Pallas kernels, local_step(): pl.pallas_call(attend_short_and_reduce, out_shape=result, in_specs=[vmem]...  45.4 us
    pallas_call x1, Pallas kernels, local_step(): pl.pallas_call(project_and_attend_long, out_shape=(sds((heads, batch, hd)...  12.9 us
    pallas_call x1, Pallas kernels, local_step(): pl.pallas_call(copy_out, out_shape=result, in_specs=[vmem] * 3, out_specs...  1.68 us

profile of v2, /device:TPU:0, one launch (start us, length us, event | category | flops | bytes accessed | tf_op | source)
XLA Modules:
  0.0 60.8 jit_solution(3822939573418121633)
XLA Ops:
  0.6 12.9 %project_and_attend_long.1 = (f32[4,256,128]{2,1,0:T(8,128)S(1)}, f32[256,128]{1,0:T(8,128)S(1)}, f32[256,128]{1,0:T(8,128)S(1)}, f32[4,256,128]{2,1,0:T(8,128)S...) custom-call(s32[256]{0:T(256)} %lens_hbm.1, ...), custom_call_target="tpu_custom_call" | custom-call | tf_op jit(solution)/shard_map/project_and_attend_long/pallas_call | solution.py:334
  13.5 45.4 %attend_short_and_reduce.1 = (bf16[256,4096]{1,0:T(8,128)(2,1)S(1)}, bf16[256,8,128]{2,1,0:T(8,128)(2,1)S(1)}, bf16[256,8,128]{2,1,0:T(8,128)(2,1)S(1)}) custom-call(f32[4,256,128]{2,1,0:T(8,128)S(1)} %get-tuple-element.14.q_ref, f32[256,128]{1,0:T(8,128)S(1)} %get-tuple-element.15.k1_ref, f32[256,128]{1,0:T(8,128)S(1)} %get-tuple-element.16.v1_ref, ...), custom_call_target="tpu_custom_call" | custom-call | tf_op jit(solution)/shard_map/attend_short_and_reduce/pallas_call | solution.py:363
  59.0 1.7 %copy_out.1 = (bf16[256,4096]{1,0:T(8,128)(2,1)}, bf16[256,8,128]{2,1,0:T(8,128)(2,1)}, bf16[256,8,128]{2,1,0:T(8,128)(2,1)}) custom-call(bf16[256,4096]{1,0:T(8,128)(2,1)S(1)} %get-tuple-element.22.y, bf16[256,8,128]{2,1,0:T(8,128)(2,1)S(1)} %get-tuple-element.23.kn, bf16[256,8,128]{2,1,0:T(8,128)(2,1)S(1)} %get-tuple-element.24.vn), custom_call_target="tpu_custom_call" | custom-call | tf_op jit(solution)/shard_map/copy_out/pallas_call | solution.py:386

commit v3 on v2

--- a/solution.py
+++ b/solution.py
@@ -10,22 +10,22 @@
 BF16 = jnp.bfloat16
 F32 = jnp.float32
 SHORT = 32
-PER_GROUP = 4
+PER_GROUP = 6
 RING = 3
 BLOCK = 256
 K_CHUNKS = 4
-BLOCK_ROWS = 64
+UNROLL = 8
 KV_STEPS = 8
 PARTS = ((0, 64), (64, 192))
-CHUNKS = tuple((32 * i, 32) for i in range(8))
+CHUNKS = ((0, 32), (32, 32), (64, 32), (96, 32), (128, 32), (160, 32), (192, 32), (224, 16), (240, 16))
 ATTEND, PROJECT, NEW = 6, 7, 8
 ORDER = (
-    (ATTEND, 0), (PROJECT, 0), (ATTEND, 1), (0, 0), (0, 1), (PROJECT, 1),
-    (0, 2), (1, 0), (0, 3), (0, 4), (NEW, 0), (0, 5), (1, 1), (0, 6), (0, 7), (NEW, 1), (2, 0), (NEW, 2),
-    (1, 2), (2, 1), (NEW, 3), (1, 3), (3, 0), (NEW, 4), (1, 4), (2, 2), (3, 1), (2, 3), (NEW, 5), (1, 5), (2, 4),
-    (3, 2), (3, 3), (NEW, 6), (1, 6), (2, 5), (3, 4), (NEW, 7), (1, 7), (2, 6), (4, 0), (3, 5), (4, 1), (5, 0),
-    (2, 7), (5, 1), (4, 2), (3, 6), (4, 3), (5, 2), (4, 4), (5, 3), (3, 7), (4, 5), (5, 4), (4, 6), (5, 5),
-    (5, 6), (4, 7), (5, 7),
+    (6, 0), (7, 0), (6, 1), (7, 1), (0, 0), (0, 1), (0, 2), (0, 3), (0, 4), (0, 5), (0, 6), (0, 7),
+    (1, 0), (0, 8), (8, 0), (1, 1), (8, 1), (8, 2), (8, 3), (2, 0), (1, 2), (8, 4), (8, 5), (2, 1),
+    (1, 3), (8, 6), (8, 7), (3, 0), (1, 4), (2, 2), (3, 1), (2, 3), (1, 5), (2, 4), (3, 2), (3, 3),
+    (1, 6), (2, 5), (1, 7), (3, 4), (1, 8), (2, 6), (4, 0), (3, 5), (2, 7), (5, 0), (4, 1), (2, 8),
+    (3, 6), (4, 2), (5, 1), (3, 7), (4, 3), (5, 2), (3, 8), (4, 4), (5, 3), (4, 5), (5, 4), (4, 6),
+    (4, 7), (5, 5), (4, 8), (5, 6), (5, 7), (5, 8),
 )
 NT = (((1,), (1,)), ((), ()))
 
@@ -33,7 +33,7 @@
 def project_and_attend_long(
     lens_hbm, x, wq, wk, wv, wo, kc, vc,
     q_out, k1_out, v1_out, ol_out, lv_out, ks_out, vs_out, wo_out,
-    xbuf, wqbuf, wkbuf, wvbuf, kbuf, vbuf, lens, idx, wsem, ksem, vsem, next_sem,
+    xbuf, wqbuf, wkbuf, wvbuf, kbuf, vbuf, ebuf, nbuf, tbuf, lens, idx, wsem, ksem, vsem, next_sem,
 ):
     me = lax.axis_index("model")
     batch = lv_out.shape[0]
@@ -58,17 +58,15 @@
     for i in range(K_CHUNKS):
         for copy in loads(i):
             copy.start()
+    vbuf[...] = jnp.zeros_like(vbuf)
     lens_load.wait()
 
     def scan(b, n):
-        length = lens[b]
         idx[n] = b
-        lv_out[pl.ds(b, 1), :] = jnp.full((1, hd), length, jnp.int32)
-        return n + (length > SHORT).astype(jnp.int32)
-
-    n_long = lax.fori_loop(0, batch, scan, jnp.int32(0), unroll=8)
+        return n + (lens[b] > SHORT).astype(jnp.int32)
+
+    n_long = lax.fori_loop(0, batch, scan, jnp.int32(0), unroll=16)
     n_groups = (n_long + PER_GROUP - 1) // PER_GROUP
-    vbuf[...] = jnp.zeros_like(vbuf)
 
     def sequence(g, j):
         return idx[jnp.maximum(jnp.minimum(g * PER_GROUP + j, n_long - 1), 0)]
@@ -96,8 +94,11 @@
         pltpu.make_async_copy(vc.at[:, me, pl.ds(0, SHORT), :], vs_out, next_sem.at[1]),
         pltpu.make_async_copy(wo, wo_out, next_sem.at[2]),
     )
-    for copy in ahead:
-        copy.start()
+    def spread(b, carry):
+        lv_out[pl.ds(b, 1), :] = jnp.full((1, hd), lens[b], jnp.int32)
+        return carry
+
+    lax.fori_loop(0, batch, spread, 0, unroll=8)
 
     for i in range(K_CHUNKS):
         for copy in loads(i):
@@ -111,6 +112,9 @@
             q_out[h] = piece if i == 0 else q_out[h] + piece
         k1_out[...] = k_part if i == 0 else k1_out[...] + k_part
         v1_out[...] = v_part if i == 0 else v1_out[...] + v_part
+    for copy in ahead:
+        copy.start()
+
     q_out[...] = q_out[...].astype(BF16).astype(F32)
     k1_out[...] = k1_out[...].astype(BF16).astype(F32)
     v1_out[...] = v1_out[...].astype(BF16).astype(F32)
@@ -118,7 +122,6 @@
     def attend(g, carry):
         slot = lax.rem(g, RING)
         each_block(g, lambda copy: copy.wait())
-        results = []
         for j in range(PER_GROUP):
             b = sequence(g, j)
             length = lens[b]
@@ -132,12 +135,18 @@
             e = jnp.exp(s - m)
             e_new = jnp.exp(s_new - m)
             total = jnp.sum(e, axis=-1, keepdims=True) + e_new
-            o = jnp.dot(e.astype(BF16), vbuf[slot, j], preferred_element_type=F32)
-            o = (o + e_new.astype(BF16).astype(F32) * v1) / total
-            results.append((row, o))
-        for row, o in results:
-            for h in range(heads):
-                ol_out[h, row, :] = o[h:h + 1, :]
+            ebuf[j] = e.astype(BF16)
+            nbuf[j] = e_new.astype(BF16).astype(F32) * v1
+            tbuf[j] = jnp.broadcast_to(total, (8, hd))
+
+        @pl.when(g < n_groups)
+        def _():
+            for j in range(PER_GROUP):
+                row = pl.ds(sequence(g, j), 1)
+                o = jnp.dot(ebuf[j], vbuf[slot, j], preferred_element_type=F32)
+                o = (o + nbuf[j]) / tbuf[j]
+                for h in range(heads):
+                    ol_out[h, row, :] = o[h:h + 1, :]
 
         @pl.when(g + RING < n_groups)
         def _():
@@ -153,7 +162,7 @@
 def attend_short_and_reduce(
     q_ref, k1_ref, v1_ref, ol_ref, lv_ref, kbuf, vbuf, wobuf, x, wk, wv,
     y_out, kn_out, vn_out,
-    xbuf, wkv, obuf, part, got_core, got_one, got_two, kvbuf,
+    xbuf, wkv, ebuf, nbuf, tbuf, obuf, part, got_core, got_one, got_two, kvbuf,
     load_sem, send_sem, recv_sem,
 ):
     me = lax.axis_index("model")
@@ -232,41 +241,45 @@
         if stage < 5:
             send(stage + 1, r).start()
 
-    def attend_block(first):
-        for g in range(BLOCK_ROWS // 8):
-            rows = pl.ds(pl.multiple_of(first + g * 8, 8), 8)
-            q = jnp.concatenate([q_ref[h, rows, :] for h in range(heads)], axis=0)
-            k1 = jnp.concatenate([k1_ref[rows, :]] * heads, axis=0)
-            v1 = jnp.concatenate([v1_ref[rows, :]] * heads, axis=0)
-            lens = jnp.concatenate([lv_ref[rows, :]] * heads, axis=0)
-            k = kbuf[rows].reshape(8 * SHORT, hd)
-            v = vbuf[rows].reshape(8 * SHORT, hd)
-            s = lax.dot_general(q.astype(BF16), k, NT, preferred_element_type=F32) * scale
-            s_new = jnp.sum(q * k1, axis=-1, keepdims=True) * scale
-            lane = lax.broadcasted_iota(jnp.int32, s.shape, 1)
-            line = lax.broadcasted_iota(jnp.int32, s.shape, 0)
-            slot = lane - (line % 8) * SHORT
-            wide = jnp.concatenate([lens] * (s.shape[1] // hd), axis=1)
-            s = jnp.where((slot >= 0) & (slot < jnp.minimum(wide, SHORT)), s, -jnp.inf)
-            m = jnp.maximum(jnp.max(s, axis=-1, keepdims=True), s_new)
-            e = jnp.exp(s - m)
-            e_new = jnp.exp(s_new - m)
-            total = jnp.sum(e, axis=-1, keepdims=True) + e_new
-            o = jnp.dot(e.astype(BF16), v, preferred_element_type=F32)
-            o = (o + e_new.astype(BF16).astype(F32) * v1) / total
-            for h in range(heads):
-                picked = jnp.where(lens[:8] > SHORT, ol_ref[h, rows, :], o[h * 8:(h + 1) * 8])
-                obuf[rows, pl.ds(h * hd, hd)] = picked
+    def weigh(group):
+        rows = pl.ds(pl.multiple_of(group * 8, 8), 8)
+        q = jnp.concatenate([q_ref[h, rows, :] for h in range(heads)], axis=0)
+        k1 = jnp.concatenate([k1_ref[rows, :]] * heads, axis=0)
+        v1 = jnp.concatenate([v1_ref[rows, :]] * heads, axis=0)
+        lens = jnp.concatenate([lv_ref[rows, :]] * heads, axis=0)
+        k = kbuf[rows].reshape(8 * SHORT, hd)
+        s = lax.dot_general(q.astype(BF16), k, NT, preferred_element_type=F32) * scale
+        s_new = jnp.sum(q * k1, axis=-1, keepdims=True) * scale
+        lane = lax.broadcasted_iota(jnp.int32, s.shape, 1)
+        line = lax.broadcasted_iota(jnp.int32, s.shape, 0)
+        slot = lane - (line % 8) * SHORT
+        wide = jnp.concatenate([lens] * (s.shape[1] // hd), axis=1)
+        s = jnp.where((slot >= 0) & (slot < jnp.minimum(wide, SHORT)), s, -jnp.inf)
+        m = jnp.maximum(jnp.max(s, axis=-1, keepdims=True), s_new)
+        e = jnp.exp(s - m)
+        e_new = jnp.exp(s_new - m)
+        total = jnp.sum(e, axis=-1, keepdims=True) + e_new
+        ebuf[group] = e.astype(BF16)
+        nbuf[group] = e_new.astype(BF16).astype(F32) * v1
+        tbuf[group] = jnp.broadcast_to(total, (8 * heads, hd))
+
+    def gather(group):
+        rows = pl.ds(pl.multiple_of(group * 8, 8), 8)
+        v = vbuf[rows].reshape(8 * SHORT, hd)
+        o = jnp.dot(ebuf[group], v, preferred_element_type=F32)
+        o = (o + nbuf[group]) / tbuf[group]
+        long = lv_ref[rows, :] > SHORT
+        for h in range(heads):
+            obuf[rows, pl.ds(h * hd, hd)] = jnp.where(long, ol_ref[h, rows, :], o[h * 8:(h + 1) * 8])
 
     def attend(first, count):
-        if count == BLOCK_ROWS:
-            attend_block(first)
-        else:
+        for act in (weigh, gather):
             def body(i, carry):
-                attend_block(first + i * BLOCK_ROWS)
+                for g in range(UNROLL):
+                    act(first // 8 + i * UNROLL + g)
                 return carry
 
-            lax.fori_loop(0, count // BLOCK_ROWS, body, 0)
+            lax.fori_loop(0, count // 8 // UNROLL, body, 0)
 
     def project_out(first, count):
         rows = pl.ds(first, count)
@@ -347,6 +360,9 @@
                 pltpu.VMEM((K_CHUNKS, depth, hd), BF16),
                 pltpu.VMEM((RING, PER_GROUP, context, hd), BF16),
                 pltpu.VMEM((RING, PER_GROUP, context, hd), BF16),
+                pltpu.VMEM((PER_GROUP, 8, context), BF16),
+                pltpu.VMEM((PER_GROUP, 8, hd), F32),
+                pltpu.VMEM((PER_GROUP, 8, hd), F32),
                 pltpu.SMEM((batch,), jnp.int32),
                 pltpu.SMEM((batch,), jnp.int32),
                 pltpu.SemaphoreType.DMA((K_CHUNKS, 5)),
@@ -354,7 +370,7 @@
                 pltpu.SemaphoreType.DMA((RING, PER_GROUP, context // BLOCK)),
                 pltpu.SemaphoreType.DMA((3,)),
             ],
-            compiler_params=pltpu.CompilerParams(vmem_limit_bytes=32 * 2**20),
+            compiler_params=pltpu.CompilerParams(vmem_limit_bytes=28 * 2**20),
             name="project_and_attend_long",
         )(lengths, x, w_query, w_key, w_value, w_out, k_cache, v_cache)
 
@@ -368,6 +384,9 @@
             scratch_shapes=[
                 pltpu.VMEM((batch, width), BF16),
                 pltpu.VMEM((width, 2 * kv_width), BF16),
+                pltpu.VMEM((batch // 8, 8 * heads, 8 * SHORT), BF16),
+                pltpu.VMEM((batch // 8, 8 * heads, hd), F32),
+                pltpu.VMEM((batch // 8, 8 * heads, hd), F32),
                 pltpu.VMEM((batch, heads * hd), F32),
                 pltpu.VMEM((8, batch, piece), F32),
                 pltpu.VMEM((4, batch, piece), F32),

time: 60.9 us -> 51.8 us (0.85)
  Pallas kernels: 60 us -> 51 us
    pallas_call x1, Pallas kernels: 45.4 us -> 38.9 us  [local_step(): pl.pallas_call(attend_short_and_reduce, out_shape=result, in_specs=[vmem]...]
    pallas_call x1, Pallas kernels: 12.9 us -> 10.4 us  [local_step(): pl.pallas_call(project_and_attend_long, out_shape=(sds((heads, batch, hd)...]
where the time goes in v3:
time: 51.8 us
  Pallas kernels  51 us (98%)
  between operations  0.81 us (2%)
    pallas_call x1, Pallas kernels, local_step(): pl.pallas_call(attend_short_and_reduce, out_shape=result, in_specs=[vmem]...  38.9 us
    pallas_call x1, Pallas kernels, local_step(): pl.pallas_call(project_and_attend_long, out_shape=(sds((heads, batch, hd)...  10.4 us
    pallas_call x1, Pallas kernels, local_step(): pl.pallas_call(copy_out, out_shape=result, in_specs=[vmem] * 3, out_specs...  1.68 us

profile of v3, /device:TPU:0, one launch (start us, length us, event | category | flops | bytes accessed | tf_op | source)
XLA Modules:
  0.0 51.8 jit_solution(12463360141858686603)
XLA Ops:
  0.6 10.4 %project_and_attend_long.1 = (f32[4,256,128]{2,1,0:T(8,128)S(1)}, f32[256,128]{1,0:T(8,128)S(1)}, f32[256,128]{1,0:T(8,128)S(1)}, f32[4,256,128]{2,1,0:T(8,128)S...) custom-call(s32[256]{0:T(256)} %lens_hbm.1, ...), custom_call_target="tpu_custom_call" | custom-call | tf_op jit(solution)/shard_map/project_and_attend_long/pallas_call | solution.py:347
  11.0 38.9 %attend_short_and_reduce.1 = (bf16[256,4096]{1,0:T(8,128)(2,1)S(1)}, bf16[256,8,128]{2,1,0:T(8,128)(2,1)S(1)}, bf16[256,8,128]{2,1,0:T(8,128)(2,1)S(1)}) custom-call(f32[4,256,128]{2,1,0:T(8,128)S(1)} %get-tuple-element.14.q_ref, f32[256,128]{1,0:T(8,128)S(1)} %get-tuple-element.15.k1_ref, f32[256,128]{1,0:T(8,128)S(1)} %get-tuple-element.16.v1_ref, ...), custom_call_target="tpu_custom_call" | custom-call | tf_op jit(solution)/shard_map/attend_short_and_reduce/pallas_call | solution.py:379
  49.9 1.7 %copy_out.1 = (bf16[256,4096]{1,0:T(8,128)(2,1)}, bf16[256,8,128]{2,1,0:T(8,128)(2,1)}, bf16[256,8,128]{2,1,0:T(8,128)(2,1)}) custom-call(bf16[256,4096]{1,0:T(8,128)(2,1)S(1)} %get-tuple-element.22.y, bf16[256,8,128]{2,1,0:T(8,128)(2,1)S(1)} %get-tuple-element.23.kn, bf16[256,8,128]{2,1,0:T(8,128)(2,1)S(1)} %get-tuple-element.24.vn), custom_call_target="tpu_custom_call" | custom-call | tf_op jit(solution)/shard_map/copy_out/pallas_call | solution.py:405

commit v4 on v3

--- a/solution.py
+++ b/solution.py
@@ -17,15 +17,15 @@
 UNROLL = 8
 KV_STEPS = 8
 PARTS = ((0, 64), (64, 192))
-CHUNKS = ((0, 32), (32, 32), (64, 32), (96, 32), (128, 32), (160, 32), (192, 32), (224, 16), (240, 16))
+CHUNKS = ((0, 64), (64, 48), (112, 48), (160, 48), (208, 32), (240, 16))
+DIRECT_SUM = ()
+DIRECT_SHARE = (4, 5)
 ATTEND, PROJECT, NEW = 6, 7, 8
 ORDER = (
-    (6, 0), (7, 0), (6, 1), (7, 1), (0, 0), (0, 1), (0, 2), (0, 3), (0, 4), (0, 5), (0, 6), (0, 7),
-    (1, 0), (0, 8), (8, 0), (1, 1), (8, 1), (8, 2), (8, 3), (2, 0), (1, 2), (8, 4), (8, 5), (2, 1),
-    (1, 3), (8, 6), (8, 7), (3, 0), (1, 4), (2, 2), (3, 1), (2, 3), (1, 5), (2, 4), (3, 2), (3, 3),
-    (1, 6), (2, 5), (1, 7), (3, 4), (1, 8), (2, 6), (4, 0), (3, 5), (2, 7), (5, 0), (4, 1), (2, 8),
-    (3, 6), (4, 2), (5, 1), (3, 7), (4, 3), (5, 2), (3, 8), (4, 4), (5, 3), (4, 5), (5, 4), (4, 6),
-    (4, 7), (5, 5), (4, 8), (5, 6), (5, 7), (5, 8),
+    (6, 0), (7, 0), (6, 1), (0, 0), (7, 1), (0, 1), (0, 2), (0, 3), (0, 4), (0, 5), (8, 0), (1, 0),
+    (8, 1), (8, 2), (8, 3), (1, 1), (8, 4), (8, 5), (8, 6), (8, 7), (2, 0), (1, 2), (2, 1), (3, 0),
+    (1, 3), (2, 2), (3, 1), (1, 4), (1, 5), (2, 3), (3, 2), (4, 0), (2, 4), (2, 5), (5, 0), (3, 3),
+    (4, 1), (3, 4), (5, 1), (3, 5), (4, 2), (5, 2), (4, 3), (4, 4), (4, 5), (5, 3), (5, 4), (5, 5),
 )
 NT = (((1,), (1,)), ((), ()))
 
@@ -173,6 +173,7 @@
     flip_y = me + 4 - 8 * py
     other_core = 1 - core
     partner = me + 1 - 2 * core
+    across = flip_x + 4 - 8 * py
     near_one = other_core * flip_x + core * flip_y
     near_two = other_core * flip_y + core * flip_x
     a = other_core * px + core * py
@@ -195,7 +196,7 @@
         copy.start()
 
     barrier = pltpu.get_barrier_semaphore()
-    for other in (partner, near_one, near_two):
+    for other in (partner, near_one, near_two, across):
         pl.semaphore_signal(barrier, inc=1, device_id={"model": other}, device_id_type=pl.DeviceIdType.MESH)
 
     def rows_of(r):
@@ -209,13 +210,20 @@
         rows = rows_of(r)
         if stage == 0:
             src, dst, other = part.at[pl.ds(4 * other_core, 4), rows], got_core.at[:, rows], partner
+        elif stage == 1 and r in DIRECT_SUM:
+            src, dst, other = part.at[base + 2 * (1 - a) + b, rows], got_one.at[0, rows], near_one
         elif stage == 1:
             src, dst, other = part.at[pl.ds(base + 2 * (1 - a), 2), rows], got_one.at[:, rows], near_one
         elif stage == 2:
             src, dst, other = part.at[base + 2 * a + 1 - b, rows], got_two.at[rows], near_two
+        elif stage == 6:
+            src, dst, other = part.at[base + 2 * (1 - a) + 1 - b, rows], got_one.at[1, rows], across
         elif stage == 3:
             src = dst = y_out.at[rows, cols_of(mine, 1)]
             other = near_two
+        elif stage == 7 or (stage == 4 and r in DIRECT_SHARE):
+            src = dst = y_out.at[rows, cols_of(mine, 1)]
+            other = across if stage == 7 else near_one
         elif stage == 4:
             src = dst = y_out.at[rows, cols_of(base + 2 * a, 2)]
             other = near_one
@@ -230,16 +238,31 @@
     def advance(stage, r):
         rows = rows_of(r)
         send(stage, r).wait()
+        following = (stage + 1,) if stage < 5 else ()
         if stage == 0:
             part[pl.ds(base, 4), rows] += got_core[:, rows]
+            if r in DIRECT_SUM:
+                following = (6, 1, 2)
         elif stage == 1:
-            part[pl.ds(base + 2 * a, 2), rows] += got_one[:, rows]
+            if r in DIRECT_SUM:
+                following = ()
+            else:
+                part[pl.ds(base + 2 * a, 2), rows] += got_one[:, rows]
         elif stage == 2:
             total = part[mine, rows] + got_two[rows]
+            if r in DIRECT_SUM:
+                send(6, r).wait()
+                total = total + (got_one[0, rows] + got_one[1, rows])
             total = total + xbuf[rows, cols_of(mine, 1)].astype(F32)
             y_out[rows, cols_of(mine, 1)] = total.astype(BF16)
-        if stage < 5:
-            send(stage + 1, r).start()
+            if r in DIRECT_SHARE:
+                following = (7, 3, 4)
+        elif stage == 3 and r in DIRECT_SHARE:
+            following = ()
+        elif stage == 4 and r in DIRECT_SHARE:
+            send(7, r).wait()
+        for later in following:
+            send(later, r).start()
 
     def weigh(group):
         rows = pl.ds(pl.multiple_of(group * 8, 8), 8)
@@ -307,7 +330,7 @@
         elif op == PROJECT:
             project_out(*PARTS[i])
             if i == 0:
-                pl.semaphore_wait(barrier, 3)
+                pl.semaphore_wait(barrier, 4)
             for r, (first, _) in enumerate(CHUNKS):
                 if PARTS[i][0] <= first < PARTS[i][0] + PARTS[i][1]:
                     send(0, r).start()
@@ -394,8 +417,8 @@
                 pltpu.VMEM((batch, piece), F32),
                 pltpu.VMEM(new_shape, F32),
                 pltpu.SemaphoreType.DMA((3,)),
-                pltpu.SemaphoreType.DMA((6, len(CHUNKS))),
-                pltpu.SemaphoreType.DMA((6, len(CHUNKS))),
+                pltpu.SemaphoreType.DMA((8, len(CHUNKS))),
+                pltpu.SemaphoreType.DMA((8, len(CHUNKS))),
             ],
             compiler_params=pltpu.CompilerParams(
                 vmem_limit_bytes=40 * 2**20, collective_id=0, has_side_effects=True

time: 51.8 us -> 49.7 us (0.959)
  Pallas kernels: 51 us -> 48.7 us
    pallas_call x1, Pallas kernels: 38.9 us -> 36.4 us  [local_step(): pl.pallas_call(attend_short_and_reduce, out_shape=result, in_specs=[vmem]...]
where the time goes in v4:
time: 49.7 us; the launch traced here: 49.5 us
  Pallas kernels  48.7 us (98%)
  between operations  0.81 us (2%)
    pallas_call x1, Pallas kernels, local_step(): pl.pallas_call(attend_short_and_reduce, out_shape=result, in_specs=[vmem]...  36.4 us
    pallas_call x1, Pallas kernels, local_step(): pl.pallas_call(project_and_attend_long, out_shape=(sds((heads, batch, hd)...  10.5 us
    pallas_call x1, Pallas kernels, local_step(): pl.pallas_call(copy_out, out_shape=result, in_specs=[vmem] * 3, out_specs...  1.68 us

profile of v4, /device:TPU:0, one launch (start us, length us, event | category | flops | bytes accessed | tf_op | source)
XLA Modules:
  0.0 49.5 jit_solution(17496832455957866885)
XLA Ops:
  0.6 10.5 %project_and_attend_long.1 = (f32[4,256,128]{2,1,0:T(8,128)S(1)}, f32[256,128]{1,0:T(8,128)S(1)}, f32[256,128]{1,0:T(8,128)S(1)}, f32[4,256,128]{2,1,0:T(8,128)S...) custom-call(s32[256]{0:T(256)} %lens_hbm.1, ...), custom_call_target="tpu_custom_call" | custom-call | tf_op jit(solution)/shard_map/project_and_attend_long/pallas_call | solution.py:370
  11.2 36.4 %attend_short_and_reduce.1 = (bf16[256,4096]{1,0:T(8,128)(2,1)S(1)}, bf16[256,8,128]{2,1,0:T(8,128)(2,1)S(1)}, bf16[256,8,128]{2,1,0:T(8,128)(2,1)S(1)}) custom-call(f32[4,256,128]{2,1,0:T(8,128)S(1)} %get-tuple-element.14.q_ref, f32[256,128]{1,0:T(8,128)S(1)} %get-tuple-element.15.k1_ref, f32[256,128]{1,0:T(8,128)S(1)} %get-tuple-element.16.v1_ref, ...), custom_call_target="tpu_custom_call" | custom-call | tf_op jit(solution)/shard_map/attend_short_and_reduce/pallas_call | solution.py:402
  47.6 1.7 %copy_out.1 = (bf16[256,4096]{1,0:T(8,128)(2,1)}, bf16[256,8,128]{2,1,0:T(8,128)(2,1)}, bf16[256,8,128]{2,1,0:T(8,128)(2,1)}) custom-call(bf16[256,4096]{1,0:T(8,128)(2,1)S(1)} %get-tuple-element.22.y, bf16[256,8,128]{2,1,0:T(8,128)(2,1)S(1)} %get-tuple-element.23.kn, bf16[256,8,128]{2,1,0:T(8,128)(2,1)S(1)} %get-tuple-element.24.vn), custom_call_target="tpu_custom_call" | custom-call | tf_op jit(solution)/shard_map/copy_out/pallas_call | solution.py:428

commit v5 on v4

--- a/solution.py
+++ b/solution.py
@@ -13,13 +13,13 @@
 PER_GROUP = 6
 RING = 3
 BLOCK = 256
-K_CHUNKS = 4
+K_CHUNKS = 2
 UNROLL = 8
 KV_STEPS = 8
 PARTS = ((0, 64), (64, 192))
 CHUNKS = ((0, 64), (64, 48), (112, 48), (160, 48), (208, 32), (240, 16))
 DIRECT_SUM = ()
-DIRECT_SHARE = (4, 5)
+DIRECT_SHARE = (3, 4, 5)
 ATTEND, PROJECT, NEW = 6, 7, 8
 ORDER = (
     (6, 0), (7, 0), (6, 1), (0, 0), (7, 1), (0, 1), (0, 2), (0, 3), (0, 4), (0, 5), (8, 0), (1, 0),

time: 49.7 us -> 50.8 us (1.022)
  Pallas kernels: 48.7 us -> 49.9 us
    pallas_call x1, Pallas kernels: 36.4 us -> 37.3 us  [local_step(): pl.pallas_call(attend_short_and_reduce, out_shape=result, in_specs=[vmem]...]
where the time goes in v5:
time: 50.8 us; the launch traced here: 50.7 us
  Pallas kernels  49.9 us (98%)
  between operations  0.81 us (2%)
    pallas_call x1, Pallas kernels, local_step(): pl.pallas_call(attend_short_and_reduce, out_shape=result, in_specs=[vmem]...  37.3 us
    pallas_call x1, Pallas kernels, local_step(): pl.pallas_call(project_and_attend_long, out_shape=(sds((heads, batch, hd)...  11 us
    pallas_call x1, Pallas kernels, local_step(): pl.pallas_call(copy_out, out_shape=result, in_specs=[vmem] * 3, out_specs...  1.68 us

profile of v5, /device:TPU:0, one launch (start us, length us, event | category | flops | bytes accessed | tf_op | source)
XLA Modules:
  0.0 50.7 jit_solution(12172827794730857747)
XLA Ops:
  0.6 11.0 %project_and_attend_long.1 = (f32[4,256,128]{2,1,0:T(8,128)S(1)}, f32[256,128]{1,0:T(8,128)S(1)}, f32[256,128]{1,0:T(8,128)S(1)}, f32[4,256,128]{2,1,0:T(8,128)S...) custom-call(s32[256]{0:T(256)} %lens_hbm.1, ...), custom_call_target="tpu_custom_call" | custom-call | tf_op jit(solution)/shard_map/project_and_attend_long/pallas_call | solution.py:370
  11.6 37.3 %attend_short_and_reduce.1 = (bf16[256,4096]{1,0:T(8,128)(2,1)S(1)}, bf16[256,8,128]{2,1,0:T(8,128)(2,1)S(1)}, bf16[256,8,128]{2,1,0:T(8,128)(2,1)S(1)}) custom-call(f32[4,256,128]{2,1,0:T(8,128)S(1)} %get-tuple-element.14.q_ref, f32[256,128]{1,0:T(8,128)S(1)} %get-tuple-element.15.k1_ref, f32[256,128]{1,0:T(8,128)S(1)} %get-tuple-element.16.v1_ref, ...), custom_call_target="tpu_custom_call" | custom-call | tf_op jit(solution)/shard_map/attend_short_and_reduce/pallas_call | solution.py:402
  48.9 1.7 %copy_out.1 = (bf16[256,4096]{1,0:T(8,128)(2,1)}, bf16[256,8,128]{2,1,0:T(8,128)(2,1)}, bf16[256,8,128]{2,1,0:T(8,128)(2,1)}) custom-call(bf16[256,4096]{1,0:T(8,128)(2,1)S(1)} %get-tuple-element.22.y, bf16[256,8,128]{2,1,0:T(8,128)(2,1)S(1)} %get-tuple-element.23.kn, bf16[256,8,128]{2,1,0:T(8,128)(2,1)S(1)} %get-tuple-element.24.vn), custom_call_target="tpu_custom_call" | custom-call | tf_op jit(solution)/shard_map/copy_out/pallas_call | solution.py:428
